TPU v7x, 32 devices: a whole 2x2x4 slice. The times are simulated.
32 devices in a mesh: fsdp: 8 (over z, y), seq: 4 (over x, core).
Axes of the slice: x: 2, y: 2, z: 4, core: 2. Of those that a mesh axis runs over, the one named last changes fastest.
Arguments:
- tokens: bfloat16 [8, 1024, 1152], P('fsdp', 'seq'), may hold values from -6 to 6
- condition: float32 [8, 1152], P('fsdp'), may hold values from -6 to 6
- w_ada: bfloat16 [1152, 6912], P('fsdp'), may hold values from -0.1875 to 0.1875
- b_ada: bfloat16 [6912], P('fsdp'), may hold values from -3 to 3
- w_qkv: bfloat16 [1152, 3456], P('fsdp'), may hold values from -0.1875 to 0.1875
- b_qv: bfloat16 [2, 1152], P(None, 'fsdp'), may hold values from -3 to 3
- w_out: bfloat16 [1152, 1152], P('fsdp'), may hold values from -0.75 to 0.75
- b_out: bfloat16 [1152], P('fsdp'), may hold values from -3 to 3
- w_up: bfloat16 [1152, 4608], P('fsdp'), may hold values from -0.1875 to 0.1875
- b_up: bfloat16 [4608], P('fsdp'), may hold values from -3 to 3
- w_down: bfloat16 [4608, 1152], P('fsdp'), may hold values from -0.09375 to 0.09375
- b_down: bfloat16 [1152], P('fsdp'), may hold values from -3 to 3
- grad_output: bfloat16 [8, 1024, 1152], P('fsdp', 'seq'), may hold values from -6 to 6
Outputs:
- output: bfloat16 [8, 1024, 1152], P('fsdp', 'seq')
- grad_tokens: bfloat16 [8, 1024, 1152], P('fsdp', 'seq')
- grad_condition: float32 [8, 1152], P('fsdp')
- grad_w_ada: float32 [1152, 6912], P('fsdp')
- grad_b_ada: float32 [6912], P('fsdp')
- grad_w_qkv: float32 [1152, 3456], P('fsdp')
- grad_b_qv: float32 [2, 1152], P(None, 'fsdp')
- grad_w_out: float32 [1152, 1152], P('fsdp')
- grad_b_out: float32 [1152], P('fsdp')
- grad_w_up: float32 [1152, 4608], P('fsdp')
- grad_b_up: float32 [4608], P('fsdp')
- grad_w_down: float32 [4608, 1152], P('fsdp')
- grad_b_down: float32 [1152], P('fsdp')
All inputs are finite; a program needn't handle non-finite values.
Results may differ from a plain program's by a relative error of at most 0.018.
Values may be sent and summed in bfloat16 or wider, within the bound.
A program may use at most 320 MiB of HBM per device.

v0:
```python
import jax
import jax.numpy as jnp
from jax import lax
from jax.sharding import PartitionSpec as P

HD = 72
EPSILON = 1e-06
GELU_C = 0.7978845608028654


def layer_norm(values):
    mean_val = jnp.mean(values, axis=-1, keepdims=True)
    centred = values - mean_val
    inv_std = lax.rsqrt(jnp.mean(centred * centred, axis=-1, keepdims=True) + EPSILON)
    return (centred * inv_std, inv_std)


def norm_back(grad_norm, normed, inv_std):
    first = jnp.mean(grad_norm, axis=-1, keepdims=True)
    second = jnp.mean(grad_norm * normed, axis=-1, keepdims=True)
    return inv_std * (grad_norm - first - normed * second)


def gelu_tanh(values):
    inner = GELU_C * (values + 0.044715 * values * values * values)
    return 0.5 * values * (1.0 + jnp.tanh(inner))


def gelu_slope(values):
    inner = GELU_C * (values + 0.044715 * values * values * values)
    tanh_val = jnp.tanh(inner)
    return 0.5 * (1.0 + tanh_val) + 0.5 * values * (1.0 - tanh_val * tanh_val) * GELU_C * (
        1.0 + 3.0 * 0.044715 * values * values
    )


def matmul(left, right):
    return jnp.dot(left, right, preferred_element_type=jnp.float32)


def matmul_tn(left, right):
    return lax.dot_general(
        left, right, (((0,), (0,)), ((), ())), preferred_element_type=jnp.float32
    )


def matmul_nt(left, right):
    return lax.dot_general(
        left, right, (((1,), (1,)), ((), ())), preferred_element_type=jnp.float32
    )


def head_scores(query, key):
    factor = HD ** (-0.5)
    return jnp.einsum("qhd,khd->hqk", query, key, preferred_element_type=jnp.float32) * factor


def attend_latent(items):
    query, key, value = items
    seq_full = query.shape[0]
    heads_here = query.shape[1] // HD
    query = query.reshape(seq_full, heads_here, HD)
    key = key.reshape(seq_full, heads_here, HD)
    value = value.reshape(seq_full, heads_here, HD)
    scores = head_scores(query, key)
    highest = jnp.max(scores, axis=-1, keepdims=True)
    log_total = highest + jnp.log(jnp.sum(jnp.exp(scores - highest), axis=-1, keepdims=True))
    probs = jnp.exp(scores - log_total).astype(jnp.bfloat16)
    mixed = jnp.einsum("hqk,khd->qhd", probs, value, preferred_element_type=jnp.float32)
    return (mixed.astype(jnp.bfloat16).reshape(seq_full, heads_here * HD), log_total)


def attend_latent_back(items):
    query, key, value, mixed, log_total, grad_mix = items
    factor = HD ** (-0.5)
    seq_full = query.shape[0]
    heads_here = query.shape[1] // HD
    shape_heads = (seq_full, heads_here, HD)
    query = query.reshape(shape_heads)
    key = key.reshape(shape_heads)
    value = value.reshape(shape_heads)
    mixed = mixed.reshape(shape_heads)
    grad_mix = grad_mix.reshape(shape_heads)
    probs = jnp.exp(head_scores(query, key) - log_total)
    delta = jnp.sum(grad_mix.astype(jnp.float32) * mixed.astype(jnp.float32), axis=-1)
    grad_probs = jnp.einsum("qhd,khd->hqk", grad_mix, value, preferred_element_type=jnp.float32)
    grad_scores = (probs * (grad_probs - jnp.transpose(delta)[:, :, None]) * factor).astype(
        jnp.bfloat16
    )
    grad_query = jnp.einsum("hqk,khd->qhd", grad_scores, key, preferred_element_type=jnp.float32)
    grad_key = jnp.einsum("hqk,qhd->khd", grad_scores, query, preferred_element_type=jnp.float32)
    grad_value = jnp.einsum(
        "hqk,qhd->khd", probs.astype(jnp.bfloat16), grad_mix, preferred_element_type=jnp.float32
    )
    flat = (seq_full, heads_here * HD)
    return (
        grad_query.astype(jnp.bfloat16).reshape(flat),
        grad_key.astype(jnp.bfloat16).reshape(flat),
        grad_value.astype(jnp.bfloat16).reshape(flat),
    )


def token_sums(values):
    return jnp.sum(values, axis=1)


def local(
    tokens,
    condition,
    w_ada,
    b_ada,
    w_qkv,
    b_qv,
    w_out,
    b_out,
    w_up,
    b_up,
    w_down,
    b_down,
    grad_output,
):
    lat_dev, seq_loc, width = tokens.shape
    row_count = lat_dev * seq_loc
    full_qkv, full_bqv, full_out, full_bout, full_up, full_bup, full_down, full_bdown, full_bada = (
        lax.all_gather(w_qkv, "fsdp", axis=0, tiled=True),
        lax.all_gather(b_qv, "fsdp", axis=1, tiled=True),
        lax.all_gather(w_out, "fsdp", axis=0, tiled=True),
        lax.all_gather(b_out, "fsdp", axis=0, tiled=True),
        lax.all_gather(w_up, "fsdp", axis=0, tiled=True),
        lax.all_gather(b_up, "fsdp", axis=0, tiled=True),
        lax.all_gather(w_down, "fsdp", axis=0, tiled=True),
        lax.all_gather(b_down, "fsdp", axis=0, tiled=True),
        lax.all_gather(b_ada, "fsdp", axis=0, tiled=True),
    )
    attn_width = full_out.shape[0]
    cond_sig = jax.nn.sigmoid(condition)
    cond_act = (condition * cond_sig).astype(jnp.bfloat16)
    full_ada = lax.all_gather(w_ada, "fsdp", axis=0, tiled=True)
    mods = matmul(cond_act, full_ada) + full_bada.astype(jnp.float32)
    mods = mods.reshape(lat_dev, 6, 1, width)
    shift_attn, scale_attn, gate_attn = (mods[:, 0], mods[:, 1], mods[:, 2])
    shift_ff, scale_ff, gate_ff = (mods[:, 3], mods[:, 4], mods[:, 5])
    source = tokens.astype(jnp.float32)
    normed1, inv1 = layer_norm(source)
    hidden1 = (
        (normed1 * (1.0 + scale_attn) + shift_attn).astype(jnp.bfloat16).reshape(row_count, width)
    )
    qkv = matmul(hidden1, full_qkv)
    tok_shape = (lat_dev, seq_loc, attn_width)
    query = (
        (qkv[:, :attn_width] + full_bqv[0].astype(jnp.float32))
        .astype(jnp.bfloat16)
        .reshape(tok_shape)
    )
    key = qkv[:, attn_width : 2 * attn_width].astype(jnp.bfloat16).reshape(tok_shape)
    value = (
        (qkv[:, 2 * attn_width :] + full_bqv[1].astype(jnp.float32))
        .astype(jnp.bfloat16)
        .reshape(tok_shape)
    )
    heads_q, heads_k, heads_v = (
        lax.all_to_all(query, "seq", split_axis=2, concat_axis=1, tiled=True),
        lax.all_to_all(key, "seq", split_axis=2, concat_axis=1, tiled=True),
        lax.all_to_all(value, "seq", split_axis=2, concat_axis=1, tiled=True),
    )
    mixed_heads, log_totals = lax.map(attend_latent, (heads_q, heads_k, heads_v))
    attn_mix = lax.all_to_all(mixed_heads, "seq", split_axis=1, concat_axis=2, tiled=True).reshape(
        row_count, attn_width
    )
    attn_out = (matmul(attn_mix, full_out) + full_bout.astype(jnp.float32)).reshape(
        lat_dev, seq_loc, width
    )
    resid1 = source + gate_attn * attn_out
    normed2, inv2 = layer_norm(resid1)
    hidden2 = (normed2 * (1.0 + scale_ff) + shift_ff).astype(jnp.bfloat16).reshape(row_count, width)
    pre_act = matmul(hidden2, full_up) + full_bup.astype(jnp.float32)
    activated = gelu_tanh(pre_act).astype(jnp.bfloat16)
    ff_out = (matmul(activated, full_down) + full_bdown.astype(jnp.float32)).reshape(
        lat_dev, seq_loc, width
    )
    output = (resid1 + gate_ff * ff_out).astype(jnp.bfloat16)
    back_qkv, back_out, back_up, back_down = (
        lax.all_gather(w_qkv, "fsdp", axis=0, tiled=True),
        lax.all_gather(w_out, "fsdp", axis=0, tiled=True),
        lax.all_gather(w_up, "fsdp", axis=0, tiled=True),
        lax.all_gather(w_down, "fsdp", axis=0, tiled=True),
    )
    grad_y = grad_output.astype(jnp.float32)
    grad_ff = (grad_y * gate_ff).reshape(row_count, width)
    grad_ff_low = grad_ff.astype(jnp.bfloat16)
    grad_w_down = matmul_tn(activated, grad_ff_low)
    grad_b_down = jnp.sum(grad_ff, axis=0)
    grad_pre = matmul_nt(grad_ff_low, back_down) * gelu_slope(pre_act)
    grad_pre_low = grad_pre.astype(jnp.bfloat16)
    grad_w_up = matmul_tn(hidden2, grad_pre_low)
    grad_b_up = jnp.sum(grad_pre, axis=0)
    grad_h2 = matmul_nt(grad_pre_low, back_up).reshape(lat_dev, seq_loc, width)
    grad_resid1 = grad_y + norm_back(grad_h2 * (1.0 + scale_ff), normed2, inv2)
    grad_attn = (grad_resid1 * gate_attn).reshape(row_count, width)
    grad_attn_low = grad_attn.astype(jnp.bfloat16)
    grad_w_out = matmul_tn(attn_mix, grad_attn_low)
    grad_b_out = jnp.sum(grad_attn, axis=0)
    grad_mix = matmul_nt(grad_attn_low, back_out).astype(jnp.bfloat16).reshape(tok_shape)
    grad_mix_heads = lax.all_to_all(grad_mix, "seq", split_axis=2, concat_axis=1, tiled=True)
    grad_qh, grad_kh, grad_vh = lax.map(
        attend_latent_back, (heads_q, heads_k, heads_v, mixed_heads, log_totals, grad_mix_heads)
    )
    grad_q, grad_k, grad_v = (
        lax.all_to_all(grad_qh, "seq", split_axis=1, concat_axis=2, tiled=True),
        lax.all_to_all(grad_kh, "seq", split_axis=1, concat_axis=2, tiled=True),
        lax.all_to_all(grad_vh, "seq", split_axis=1, concat_axis=2, tiled=True),
    )
    grad_qkv = jnp.concatenate([grad_q, grad_k, grad_v], axis=2).reshape(row_count, 3 * attn_width)
    grad_w_qkv = matmul_tn(hidden1, grad_qkv)
    grad_b_qv = jnp.stack(
        [
            jnp.sum(grad_q.astype(jnp.float32), axis=(0, 1)),
            jnp.sum(grad_v.astype(jnp.float32), axis=(0, 1)),
        ]
    )
    grad_h1 = matmul_nt(grad_qkv, back_qkv).reshape(lat_dev, seq_loc, width)
    grad_tokens = (grad_resid1 + norm_back(grad_h1 * (1.0 + scale_attn), normed1, inv1)).astype(
        jnp.bfloat16
    )
    grad_mods = jnp.stack(
        [
            token_sums(grad_h1),
            token_sums(grad_h1 * normed1),
            token_sums(grad_resid1 * attn_out),
            token_sums(grad_h2),
            token_sums(grad_h2 * normed2),
            token_sums(grad_y * ff_out),
        ],
        axis=1,
    )
    grad_mods_low = grad_mods.reshape(lat_dev, 6 * width).astype(jnp.bfloat16)
    grad_b_ada = jnp.sum(grad_mods_low.astype(jnp.float32), axis=0)
    grad_w_ada = lax.psum_scatter(
        matmul_tn(cond_act, grad_mods_low).astype(jnp.bfloat16),
        "fsdp",
        scatter_dimension=0,
        tiled=True,
    )
    grad_cond_act = matmul_nt(grad_mods_low, full_ada)
    grad_cond_part = grad_cond_act * cond_sig * (1.0 + condition * (1.0 - cond_sig))
    s_wqkv, s_bqv, s_wout, s_bout, s_wup, s_bup, s_wdown, s_bdown, s_bada = (
        lax.psum_scatter(grad_w_qkv, ("fsdp", "seq"), scatter_dimension=0, tiled=True),
        lax.psum_scatter(grad_b_qv, ("fsdp", "seq"), scatter_dimension=1, tiled=True),
        lax.psum_scatter(grad_w_out, ("fsdp", "seq"), scatter_dimension=0, tiled=True),
        lax.psum_scatter(grad_b_out, ("fsdp", "seq"), scatter_dimension=0, tiled=True),
        lax.psum_scatter(grad_w_up, ("fsdp", "seq"), scatter_dimension=0, tiled=True),
        lax.psum_scatter(grad_b_up, ("fsdp", "seq"), scatter_dimension=0, tiled=True),
        lax.psum_scatter(grad_w_down, ("fsdp", "seq"), scatter_dimension=0, tiled=True),
        lax.psum_scatter(grad_b_down, ("fsdp", "seq"), scatter_dimension=0, tiled=True),
        lax.psum_scatter(grad_b_ada, ("fsdp", "seq"), scatter_dimension=0, tiled=True),
    )
    t_wqkv, t_bqv, t_wout, t_bout, t_wup, t_bup, t_wdown, t_bdown, t_bada = (
        lax.all_gather(s_wqkv.astype(jnp.bfloat16), "seq", axis=0, tiled=True).astype(s_wqkv.dtype),
        lax.all_gather(s_bqv.astype(jnp.bfloat16), "seq", axis=1, tiled=True).astype(s_bqv.dtype),
        lax.all_gather(s_wout.astype(jnp.bfloat16), "seq", axis=0, tiled=True).astype(s_wout.dtype),
        lax.all_gather(s_bout.astype(jnp.bfloat16), "seq", axis=0, tiled=True).astype(s_bout.dtype),
        lax.all_gather(s_wup.astype(jnp.bfloat16), "seq", axis=0, tiled=True).astype(s_wup.dtype),
        lax.all_gather(s_bup.astype(jnp.bfloat16), "seq", axis=0, tiled=True).astype(s_bup.dtype),
        lax.all_gather(s_wdown.astype(jnp.bfloat16), "seq", axis=0, tiled=True).astype(
            s_wdown.dtype
        ),
        lax.all_gather(s_bdown.astype(jnp.bfloat16), "seq", axis=0, tiled=True).astype(
            s_bdown.dtype
        ),
        lax.all_gather(s_bada.astype(jnp.bfloat16), "seq", axis=0, tiled=True).astype(s_bada.dtype),
    )
    t_wada, t_cond = (
        lax.psum(grad_w_ada, "seq").astype(jnp.float32),
        lax.psum(grad_cond_part.astype(jnp.bfloat16), "seq").astype(jnp.float32),
    )
    return (
        output,
        grad_tokens,
        t_cond,
        t_wada,
        t_bada,
        t_wqkv,
        t_bqv,
        t_wout,
        t_bout,
        t_wup,
        t_bup,
        t_wdown,
        t_bdown,
    )


def solution(mesh):
    in_specs = (
        P("fsdp", "seq", None),
        P("fsdp", None),
        P("fsdp", None),
        P("fsdp"),
        P("fsdp", None),
        P(None, "fsdp"),
        P("fsdp", None),
        P("fsdp"),
        P("fsdp", None),
        P("fsdp"),
        P("fsdp", None),
        P("fsdp"),
        P("fsdp", "seq", None),
    )
    out_specs = (
        P("fsdp", "seq", None),
        P("fsdp", "seq", None),
        P("fsdp", None),
        P("fsdp", None),
        P("fsdp"),
        P("fsdp", None),
        P(None, "fsdp"),
        P("fsdp", None),
        P("fsdp"),
        P("fsdp", None),
        P("fsdp"),
        P("fsdp", None),
        P("fsdp"),
    )
    return jax.shard_map(local, mesh=mesh, in_specs=in_specs, out_specs=out_specs, check_vma=False)
```

profile of v0, /device:TPU:0, one launch (start us, length us, event | category | flops | bytes accessed | tf_op | source)
XLA Modules:
  0.0 1821.9 jit_solution(10421692875912982630)
XLA Ops:
  13.2 22.8 %all-gather = bf16[8,144,2]{1,2,0:T(2,128)(2,1)S(1)} all-gather(bf16[1,144,2]{1,2,0:T(2,128)(2,1)S(1)} %bitcast.233), channel_id=1, replica_groups=mesh['fsdp'=8,'seq'=4] {'fsdp'}, dimensions={0}, use_global_device_ids=true | all-gather | bytes 5184 | tf_op jit(solution)/shard_map/all_gather | solution.py:126
  37.1 36.0 %all-reduce.20 = (bf16[6912]{0:T(1024)(128)(2,1)S(1)}, bf16[1152]{0:T(1024)(128)(2,1)}, bf16[1152]{0:T(1024)(128)(2,1)}, bf16[4608]{0:T(1024)(128)(2,1)}) all-reduce(bf16[6912]{0:T(1024)(128)(2,1)S(1)} %dynamic-update-slice, bf16[1152]{0:T(1024)(128)(2,1)S(1)} %dynamic-update-slice.1, ...), channel_id=1, replica_groups=mesh['fsdp'=8,'seq'=4] {'fsdp'}, use_global_device_ids=true, to_apply=%add | all-reduce | flops 13824 | bytes 55296
  73.7 156.8 %all-gather.13.cloned.1.call-done = bf16[1152,6912]{1,0:T(8,128)(2,1)} async-done(((bf16[144,6912]{1,0:T(8,128)(2,1)}), bf16[1152,6912]{1,0:T(8,128)(2,1)}) %all-gather.13.cloned.1.call-update) | async-done | bytes 15925264 | tf_op jit(solution)/shard_map/all_gather | solution.py:138
  230.4 7.7 convolution_reduce_fusion
  238.9 111.1 %all-gather.15.cloned.1.call-done = bf16[1152,3456]{1,0:T(8,128)(2,1)} async-done(((bf16[144,3456]{1,0:T(8,128)(2,1)}), bf16[1152,3456]{1,0:T(8,128)(2,1)}) %all-gather.15.cloned.1.call-update) | async-done | bytes 7962640 | tf_op jit(solution)/shard_map/all_gather | solution.py:125
  350.0 6.0 fusion.74
  360.4 6.2 reduce.42
  373.3 6.2 reduce.43
  387.6 6.2 reduce.44
  402.3 6.4 all-to-all-done.2
  411.9 8.5 multiply_reduce_fusion
  420.4 8.6 exponential_reduce_fusion
  429.0 9.6 convolution_convert_fusion.4
  442.9 6.5 reduce.45
  458.2 8.3 all-to-all-done.3
  480.4 77.7 %all-gather.19.cloned.1.call-done = bf16[1152,4608]{1,0:T(8,128)(2,1)} async-done(((bf16[144,4608]{1,0:T(8,128)(2,1)}), bf16[1152,4608]{1,0:T(8,128)(2,1)}) %all-gather.19.cloned.1.call-update) | async-done | bytes 10616848 | tf_op jit(solution)/shard_map/all_gather | solution.py:129
  558.1 6.2 convolution_add_fusion
  566.7 9.3 fusion.52
  577.3 133.2 %all-gather.21.cloned.1.call-done = bf16[4608,1152]{1,0:T(8,128)(2,1)} async-done(((bf16[576,1152]{1,0:T(8,128)(2,1)}), bf16[4608,1152]{1,0:T(8,128)(2,1)}) %all-gather.21.cloned.1.call-update) | async-done | bytes 10616848 | tf_op jit(solution)/shard_map/all_gather | solution.py:131
  710.4 8.9 fusion.85
  719.4 9.7 fusion.34
  729.9 10.6 fusion.18
  747.2 8.1 reduce.46
  757.4 13.9 all_to_all.129
  780.1 9.7 convolution_convert_fusion.1
  794.3 7.4 reduce.47
  811.2 11.1 multiply_convert_fusion.1
  830.5 7.4 reduce.48
  845.6 5.4 convolution_convert_fusion.3
  853.9 6.5 reduce.49
  900.7 7.3 fusion.29
  914.5 6.6 multiply_convert_fusion
  926.2 9.3 fusion.39
  935.6 8.1 fusion.43
  943.7 577.3 %fusion.80 = (f32[48,3456]{1,0:T(8,128)S(1)}, f32[48,1152]{1,0:T(8,128)S(1)}, f32[40,4608]{1,0:T(8,128)S(1)}) fusion(f32[1152,3456]{1,0:T(8,128)} %fusion.43, f32[1152,1152]{1,0:T(8,128)} %fusion.57, f32[1152,4608]{1,0:T(8,128)} %fusion.39), kind=kCustom, calls=%all-reduce-scatter.3 | all-reduce-scatter fusion | flops 12976130 | bytes 44089344
  1523.8 35.3 %collective-permute-start.17 = (bf16[40,4608]{1,0:T(8,128)(2,1)}, bf16[40,4608]{1,0:T(8,128)(2,1)}, u32[]{:S(2)}, u32[]{:S(2)}) collective-permute-start(bf16[40,4608]{1,0:T(8,128)(2,1)} %convert.54), channel_id=1, source_target_pairs={{0,2},{1,3},{2,4},{3,5},{4,6},{5,7},{6,8},{7,9},{8,10},{9,11},{10,... | collective-permute-start | bytes 1105928
  1563.7 9.3 collective-permute-done.19
  1573.0 16.8 concatenate.12
  1595.8 6.9 collective-permute-start.14
  1604.9 5.7 collective-permute-start.12
  1623.2 9.8 fusion.11
  1633.1 39.2 %all-reduce.19 = (bf16[6912]{0:T(1024)(128)(2,1)S(1)}, bf16[2,1152]{1,0:T(2,128)(2,1)S(1)}, bf16[1152]{0:T(1024)(128)(2,1)S(1)}, bf16[4608]{0:T(1024)(128)(2,1)S(1)}, bf16[1152]{0:T(1024)(128)(2,1)S(1)}) all-reduce(bf16[6912]{0:T(1024)(128)(2,1)S(1)} %copy-done.22, ...), channel_id=3, replica_groups=mesh['fsdp'=8,'seq'=4] {'fsdp','seq'}, use_global_device_ids=true, to_apply=%region_20.21.clone | all-reduce | flops 16128 | bytes 82944
  1686.7 5.0 all-gather.2
  1697.8 7.6 all-reduce.21
  1714.9 5.3 concatenate.11
  1729.7 27.9 %all-gather.3 = bf16[4,36,1152]{2,1,0:T(8,128)(2,1)S(1)} all-gather(bf16[1,36,1152]{2,1,0:T(8,128)(2,1)S(1)} %fusion.60), channel_id=1, replica_groups=mesh['fsdp'=8,'seq'=4] {'seq'}, dimensions={0}, use_global_device_ids=true | all-gather | bytes 414720 | tf_op jit(solution)/shard_map/all_gather | solution.py:260
  1758.6 33.7 %concatenate.10 = bf16[420,3456]{1,0:T(8,128)(2,1)} concatenate(bf16[36,3456]{1,0:T(8,128)(2,1)} %collective-permute-done.7, bf16[48,3456]{1,0:T(8,128)(2,1)S(1)} %collective-permute-done.6, bf16[48,3456]{1,0:T(8,128)(2,1)} %copy-done.18, bf16[48,3456]{1,0:T(8,128)(2,1)} %collective-permute-done.4, bf16[48,3456]{1,0:T(8,128)(2,1)} %collective-permute-done.3, ...), dimensions={0} | concatenate | bytes 6137856
  1793.4 10.4 all-gather.1
  (339 shorter events, 248.7 us)
Async XLA Ops:
  7.2 223.3 %all-gather.13.cloned.1.call-start = ((), (), s32[]{:S(2)}) async-start(), calls=%async_computation.10 | async-start | bytes 17915904 | tf_op jit(solution)/shard_map/all_gather | solution.py:138
  7.9 28.2 %copy-start.57 = (bf16[144]{0:T(256)(128)(2,1)S(1)}, bf16[144]{0:T(256)(128)(2,1)}, u32[]{:S(2)}) copy-start(bf16[144]{0:T(256)(128)(2,1)} %param.20) | copy-start | bytes 868
  7.9 28.4 %copy-start.58 = (bf16[144]{0:T(256)(128)(2,1)S(1)}, bf16[144]{0:T(256)(128)(2,1)}, u32[]{:S(2)}) copy-start(bf16[144]{0:T(256)(128)(2,1)} %param.24) | copy-start | bytes 868
  8.0 28.7 %copy-start.54 = (bf16[864]{0:T(1024)(128)(2,1)S(1)}, bf16[864]{0:T(1024)(128)(2,1)}, u32[]{:S(2)}) copy-start(bf16[864]{0:T(1024)(128)(2,1)} %param.16) | copy-start | bytes 5188
  8.0 28.9 %copy-start.55 = (bf16[576]{0:T(1024)(128)(2,1)S(1)}, bf16[576]{0:T(1024)(128)(2,1)}, u32[]{:S(2)}) copy-start(bf16[576]{0:T(1024)(128)(2,1)} %param.22) | copy-start | bytes 3460
  8.0 65.2 %copy-start.1 = (bf16[1,256,1152]{2,1,0:T(8,128)(2,1)S(1)}, bf16[1,256,1152]{2,1,0:T(8,128)(2,1)}, u32[]{:S(2)}) copy-start(bf16[1,256,1152]{2,1,0:T(8,128)(2,1)} %param.13) | copy-start | bytes 1769476
  8.0 342.0 %all-gather.15.cloned.1.call-start = ((), (), s32[]{:S(2)}) async-start(), calls=%async_computation.11 | async-start | bytes 8957952 | tf_op jit(solution)/shard_map/all_gather | solution.py:125
  8.7 466.4 %all-gather.17.cloned.1.call-start = ((), (), s32[]{:S(2)}) async-start(), calls=%async_computation.12 | async-start | bytes 2985984 | tf_op jit(solution)/shard_map/all_gather | solution.py:127
  9.5 221.0 %copy-start.28 = (f32[1,1152]{1,0:T(1,128)S(1)}, f32[1,1152]{1,0:T(1,128)}, u32[]{:S(2)}) copy-start(f32[1,1152]{1,0:T(1,128)} %param.14) | copy-start | bytes 13828
  9.5 548.6 %all-gather.19.cloned.1.call-start = ((), (), s32[]{:S(2)}) async-start(), calls=%async_computation.13 | async-start | bytes 11943936 | tf_op jit(solution)/shard_map/all_gather | solution.py:129
  10.1 700.4 %all-gather.21.cloned.1.call-start = ((), (), s32[]{:S(2)}) async-start(), calls=%async_computation.14 | async-start | bytes 11943936 | tf_op jit(solution)/shard_map/all_gather | solution.py:131
  73.3 276.6 %copy-start.36 = (f32[256]{0:T(256)}, f32[256]{0:T(256)S(1)}, u32[]{:S(2)}) copy-start(f32[256]{0:T(256)S(1)} %broadcast_multiply_fusion.5) | copy-start | bytes 3076
  73.6 276.3 %copy-start.43 = (f32[256]{0:T(256)}, f32[256]{0:T(256)S(1)}, u32[]{:S(2)}) copy-start(f32[256]{0:T(256)S(1)} %add_rsqrt_fusion.1) | copy-start | bytes 3076
  238.9 117.1 %copy-start.25 = (f32[1152]{0:T(1024)}, f32[1152]{0:T(1024)S(1)}, u32[]{:S(2)}) copy-start(f32[1152]{0:T(1024)S(1)} %get-tuple-element.76) | copy-start | bytes 13828
  367.5 13.1 all-to-all-start
  380.6 14.1 all-to-all-start.1
  394.7 13.9 all-to-all-start.2
  400.7 28.3 %copy-start.10 = (bf16[1024,4,72]{0,2,1:T(8,128)(2,1)}, bf16[1024,4,72]{0,2,1:T(8,128)(2,1)S(1)}, u32[]{:S(2)}) copy-start(bf16[1024,4,72]{0,2,1:T(8,128)(2,1)S(1)} %reshape.384) | copy-start | bytes 1769476
  452.8 13.7 all-to-all-start.3
  457.0 1161.4 %reduce-scatter.12.cloned.1.call-start = ((), (), s32[]{:S(2)}) async-start(), calls=%async_computation.17 | async-start | bytes 21897216 | tf_op jit(solution)/shard_map/reduce_scatter | solution.py:253
  805.2 36.1 %all-to-all-start.7 = ((bf16[4,2,36864]{2,1,0:T(2,128)(2,1)}), bf16[4,2,36864]{2,1,0:T(2,128)(2,1)}, u32[]{:S(2)}, u32[]{:S(2)}) async-start(bf16[4,2,36864]{2,1,0:T(2,128)(2,1)} %reshape.483), calls=%async_computation.7 | async-start | bytes 1179648 | tf_op jit(solution)/shard_map/all_to_all | solution.py:211
  841.3 21.1 %all-to-all-start.6 = ((bf16[4,2,36864]{2,1,0:T(2,128)(2,1)}), bf16[4,2,36864]{2,1,0:T(2,128)(2,1)}, u32[]{:S(2)}, u32[]{:S(2)}) async-start(bf16[4,2,36864]{2,1,0:T(2,128)(2,1)} %reshape.485), calls=%async_computation.6 | async-start | bytes 1179648 | tf_op jit(solution)/shard_map/all_to_all | solution.py:210
  862.3 27.8 %all-to-all-start.5 = ((bf16[4,2,36864]{2,1,0:T(2,128)(2,1)}), bf16[4,2,36864]{2,1,0:T(2,128)(2,1)}, u32[]{:S(2)}, u32[]{:S(2)}) async-start(bf16[4,2,36864]{2,1,0:T(2,128)(2,1)} %reshape.487), calls=%async_computation.5 | async-start | bytes 1179648 | tf_op jit(solution)/shard_map/all_to_all | solution.py:209
  866.5 853.7 %reduce-scatter.10.cloned.1.call-start = ((), (), s32[]{:S(2)}) async-start(), calls=%async_computation.15 | async-start | bytes 17915904 | tf_op jit(solution)/shard_map/reduce_scatter | solution.py:238
  921.1 884.0 %all-gather.25.cloned.1.call-start = ((), (), s32[]{:S(2)}) async-start(), calls=%async_computation.19 | async-start | bytes 1843200 | tf_op jit(solution)/shard_map/all_gather | solution.py:262
  1521.8 51.2 %collective-permute-start.18 = (bf16[40,4608]{1,0:T(8,128)(2,1)}, bf16[40,4608]{1,0:T(8,128)(2,1)}, u32[]{:S(2)}, u32[]{:S(2)}) collective-permute-start(bf16[40,4608]{1,0:T(8,128)(2,1)} %convert.54), channel_id=1, source_target_pairs={{0,3},{1,4},{2,5},{3,6},{4,7},{5,8},{6,9},{7,10},{8,11},{9,12},{10... | collective-permute-start | bytes 1105928
  1523.8 49.2 %collective-permute-start.17 = (bf16[40,4608]{1,0:T(8,128)(2,1)}, bf16[40,4608]{1,0:T(8,128)(2,1)}, u32[]{:S(2)}, u32[]{:S(2)}) collective-permute-start(bf16[40,4608]{1,0:T(8,128)(2,1)} %convert.54), channel_id=1, source_target_pairs={{0,2},{1,3},{2,4},{3,5},{4,6},{5,7},{6,8},{7,9},{8,10},{9,11},{10,... | collective-permute-start | bytes 1105928
  1559.1 13.9 collective-permute-start.16
  1562.2 10.8 collective-permute-start.19
  1563.6 28.1 %copy-start.59 = (u32[32]{0:T(128)S(1)}, u32[32]{0:T(128)}, u32[]{:S(2)}) copy-start(u32[32]{0:T(128)} %constant.92) | copy-start | bytes 388
  1591.7 216.2 %all-gather.23.cloned.1.call-start = ((), (), s32[]{:S(2)}) async-start(), calls=%async_computation.18 | async-start | bytes 1658880 | tf_op jit(solution)/shard_map/all_gather | solution.py:264
  1595.8 80.7 %collective-permute-start.14 = (bf16[48,1152]{1,0:T(8,128)(2,1)S(1)}, bf16[48,1152]{1,0:T(8,128)(2,1)S(1)}, u32[]{:S(2)}, u32[]{:S(2)}) collective-permute-start(bf16[48,1152]{1,0:T(8,128)(2,1)S(1)} %convert.56), channel_id=1, source_target_pairs={{0,7},{1,8},{2,9},{3,10},{4,11},{5,12},{6,13},{7,14},{8,15},{9,16}... | collective-permute-start | bytes 331784
  1602.7 78.8 %collective-permute-start.13 = (bf16[48,1152]{1,0:T(8,128)(2,1)S(1)}, bf16[48,1152]{1,0:T(8,128)(2,1)}, u32[]{:S(2)}, u32[]{:S(2)}) collective-permute-start(bf16[48,1152]{1,0:T(8,128)(2,1)S(1)} %convert.56), channel_id=1, source_target_pairs={{0,6},{1,7},{2,8},{3,9},{4,10},{5,11},{6,12},{7,13},{8,14},{9,15},... | collective-permute-start | bytes 331784
  1604.9 77.9 %collective-permute-start.12 = (bf16[48,1152]{1,0:T(8,128)(2,1)S(1)}, bf16[48,1152]{1,0:T(8,128)(2,1)}, u32[]{:S(2)}, u32[]{:S(2)}) collective-permute-start(bf16[48,1152]{1,0:T(8,128)(2,1)S(1)} %convert.56), channel_id=1, source_target_pairs={{0,5},{1,6},{2,7},{3,8},{4,9},{5,10},{6,11},{7,12},{8,13},{9,14},{... | collective-permute-start | bytes 331784
  1611.8 111.7 %collective-permute-start.6 = (bf16[48,3456]{1,0:T(8,128)(2,1)S(1)}, bf16[48,3456]{1,0:T(8,128)(2,1)S(1)}, u32[]{:S(2)}, u32[]{:S(2)}) collective-permute-start(bf16[48,3456]{1,0:T(8,128)(2,1)S(1)} %convert.55), channel_id=1, source_target_pairs={{0,7},{1,8},{2,9},{3,10},{4,11},{5,12},{6,13},{7,14},{8,15},{9,16}... | collective-permute-start | bytes 995336
  1613.1 59.2 %collective-permute-start.15 = (bf16[36,1152]{1,0:T(8,128)(2,1)}, bf16[36,1152]{1,0:T(8,128)(2,1)S(1)}, u32[]{:S(2)}, u32[]{:S(2)}) collective-permute-start(bf16[36,1152]{1,0:T(8,128)(2,1)} %slice.57), channel_id=1, source_target_pairs={{0,8},{1,9},{2,10},{3,11},{4,12},{5,13},{6,14},{7,15},{8,16},{9,17... | collective-permute-start | bytes 248840
  1620.2 190.6 %all-reduce.25.cloned.1.call-start = ((), (), s32[]{:S(2)}) async-start(), calls=%async_computation.16 | async-start | bytes 3981312 | tf_op jit(solution)/shard_map/psum | solution.py:273
  1672.3 55.3 %collective-permute-start.5 = (bf16[48,3456]{1,0:T(8,128)(2,1)S(1)}, bf16[48,3456]{1,0:T(8,128)(2,1)S(1)}, u32[]{:S(2)}, u32[]{:S(2)}) collective-permute-start(bf16[48,3456]{1,0:T(8,128)(2,1)S(1)} %convert.55), channel_id=1, source_target_pairs={{0,6},{1,7},{2,8},{3,9},{4,10},{5,11},{6,12},{7,13},{8,14},{9,15},... | collective-permute-start | bytes 995336
  1676.5 15.3 collective-permute-start.11
  1681.5 12.9 collective-permute-start.10
  1682.8 37.5 %collective-permute-start.7 = (bf16[36,3456]{1,0:T(8,128)(2,1)}, bf16[36,3456]{1,0:T(8,128)(2,1)}, u32[]{:S(2)}, u32[]{:S(2)}) collective-permute-start(bf16[36,3456]{1,0:T(8,128)(2,1)} %slice.56), channel_id=1, source_target_pairs={{0,8},{1,9},{2,10},{3,11},{4,12},{5,13},{6,14},{7,15},{8,16},{9,17... | collective-permute-start | bytes 746504
  1691.8 17.2 collective-permute-start.9
  1694.4 16.6 collective-permute-start.8
  1709.0 49.6 %collective-permute-start.4 = (bf16[48,3456]{1,0:T(8,128)(2,1)S(1)}, bf16[48,3456]{1,0:T(8,128)(2,1)}, u32[]{:S(2)}, u32[]{:S(2)}) collective-permute-start(bf16[48,3456]{1,0:T(8,128)(2,1)S(1)} %convert.55), channel_id=1, source_target_pairs={{0,5},{1,6},{2,7},{3,8},{4,9},{5,10},{6,11},{7,12},{8,13},{9,14},{... | collective-permute-start | bytes 995336
  1711.6 47.0 %collective-permute-start.3 = (bf16[48,3456]{1,0:T(8,128)(2,1)S(1)}, bf16[48,3456]{1,0:T(8,128)(2,1)}, u32[]{:S(2)}, u32[]{:S(2)}) collective-permute-start(bf16[48,3456]{1,0:T(8,128)(2,1)S(1)} %convert.55), channel_id=1, source_target_pairs={{0,4},{1,5},{2,6},{3,7},{4,8},{5,9},{6,10},{7,11},{8,12},{9,13},{1... | collective-permute-start | bytes 995336
  1720.3 38.3 %collective-permute-start.2 = (bf16[48,3456]{1,0:T(8,128)(2,1)S(1)}, bf16[48,3456]{1,0:T(8,128)(2,1)S(1)}, u32[]{:S(2)}, u32[]{:S(2)}) collective-permute-start(bf16[48,3456]{1,0:T(8,128)(2,1)S(1)} %convert.55), channel_id=1, source_target_pairs={{0,3},{1,4},{2,5},{3,6},{4,7},{5,8},{6,9},{7,10},{8,11},{9,12},{10... | collective-permute-start | bytes 995336
  1723.5 35.1 %collective-permute-start.1 = (bf16[48,3456]{1,0:T(8,128)(2,1)S(1)}, bf16[48,3456]{1,0:T(8,128)(2,1)}, u32[]{:S(2)}, u32[]{:S(2)}) collective-permute-start(bf16[48,3456]{1,0:T(8,128)(2,1)S(1)} %convert.55), channel_id=1, source_target_pairs={{0,2},{1,3},{2,4},{3,5},{4,6},{5,7},{6,8},{7,9},{8,10},{9,11},{10,... | collective-permute-start | bytes 995336
  1727.7 30.9 %collective-permute-start = (bf16[48,3456]{1,0:T(8,128)(2,1)S(1)}, bf16[48,3456]{1,0:T(8,128)(2,1)}, u32[]{:S(2)}, u32[]{:S(2)}) collective-permute-start(bf16[48,3456]{1,0:T(8,128)(2,1)S(1)} %convert.55), channel_id=1, source_target_pairs={{0,1},{1,2},{2,3},{3,4},{4,5},{5,6},{6,7},{7,8},{8,9},{9,10},{10,1... | collective-permute-start | bytes 995336
  (50 other events, 449.9 us)
Sparse Core Ops, SparseCore 0:
  10.2 220.2 all-gather.12
  232.6 117.2 all-gather.14
  352.1 53.1 all-gather.16
  407.4 150.6 all-gather.18
  560.1 150.2 all-gather.20
  716.7 223.6 reduce-scatter.11
  944.3 462.4 reduce-scatter.9
  1591.8 24.0 all-gather.24
  1620.4 22.4 all-gather.22
  1720.4 62.1 all-reduce.24
where the time goes:
time: 1840 us; the launch traced here: 1820 us
  blocking collectives  740 us (40%)
  waiting for transfers between devices  506 us (28%)
  local copies, waits for them, and re-layouts  184 us (10%)
  matrix products  152 us (8%)
  starting transfers between devices  124 us (7%)
  other arithmetic  95.9 us (5%)
  between operations  19.8 us (1%)
    unnamed x3, blocking collectives  653 us
    all_gather x1, waiting for transfers between devices, local(): full_ada = lax.all_gather(w_ada, 'fsdp', axis=0, tiled=True)  157 us
    all_gather x1, waiting for transfers between devices, local(): lax.all_gather(w_down, 'fsdp', axis=0, tiled=True)  133 us
    unnamed x177, local copies, waits for them, and re-layouts  114 us
    all_gather x1, waiting for transfers between devices, local(): lax.all_gather(w_qkv, 'fsdp', axis=0, tiled=True)  111 us
    unnamed x20, starting transfers between devices  95.3 us
    all_gather x1, waiting for transfers between devices, local(): lax.all_gather(w_up, 'fsdp', axis=0, tiled=True)  77.7 us
    unnamed x11, other arithmetic  55.2 us
  transfers between devices with their start and end apart: 37, of which 8 were waited for; matrix products, arithmetic and copies ran while one was open for 54% of the time, Pallas kernels for 0%

commit v1 on v0

--- a/solution.py
+++ b/solution.py
@@ -122,7 +122,9 @@
     lat_dev, seq_loc, width = tokens.shape
     row_count = lat_dev * seq_loc
     full_qkv, full_bqv, full_out, full_bout, full_up, full_bup, full_down, full_bdown, full_bada = (
-        lax.all_gather(w_qkv, "fsdp", axis=0, tiled=True),
+        jnp.concatenate(
+            lax.all_to_all(jnp.stack([w_qkv] * lax.axis_size("fsdp")), "fsdp", 0, 0), axis=0
+        ),
         lax.all_gather(b_qv, "fsdp", axis=1, tiled=True),
         lax.all_gather(w_out, "fsdp", axis=0, tiled=True),
         lax.all_gather(b_out, "fsdp", axis=0, tiled=True),

time: 1840 us -> 1910 us (1.038)
  blocking collectives: 740 us -> 1130 us
  waiting for transfers between devices: 506 us -> 201 us
    all_gather x1, blocking collectives: 22.8 us -> 222 us  [local(): lax.all_gather(b_qv, 'fsdp', axis=1, tiled=True)]
    unnamed x3, blocking collectives: 653 us -> 843 us
    all_gather x1, waiting for transfers between devices: 157 us -> 0.02 us  [local(): full_ada = lax.all_gather(w_ada, 'fsdp', axis=0, tiled=True)]
    all_gather x1, waiting for transfers between devices: 111 us -> 0.01 us  [local(): lax.all_gather(w_qkv, 'fsdp', axis=0, tiled=True)]
    all_gather x1, waiting for transfers between devices: 77.7 us -> 46.7 us  [local(): lax.all_gather(w_up, 'fsdp', axis=0, tiled=True)]
    unnamed x20, starting transfers between devices: 95.3 us -> 73.4 us
  transfers between devices with their start and end apart: 37 -> 38, of which waited for: 8 -> 7; matrix products, arithmetic and copies ran while one was open for 54% -> 56% of each run, Pallas kernels for 0% -> 0%
where the time goes in v1:
time: 1910 us; the launch traced here: 1890 us
  blocking collectives  1130 us (59%)
  waiting for transfers between devices  201 us (11%)
  local copies, waits for them, and re-layouts  188 us (10%)
  matrix products  149 us (8%)
  starting transfers between devices  110 us (6%)
  other arithmetic  96.5 us (5%)
  between operations  19.8 us (1%)
    unnamed x3, blocking collectives  843 us
    all_gather x1, blocking collectives, local(): lax.all_gather(b_qv, 'fsdp', axis=1, tiled=True)  222 us
    all_gather x1, waiting for transfers between devices, local(): lax.all_gather(w_down, 'fsdp', axis=0, tiled=True)  133 us
    unnamed x177, local copies, waits for them, and re-layouts  113 us
    unnamed x20, starting transfers between devices  73.4 us
    unnamed x11, other arithmetic  55.8 us
    all_gather x1, waiting for transfers between devices, local(): lax.all_gather(w_up, 'fsdp', axis=0, tiled=True)  46.7 us
  transfers between devices with their start and end apart: 38, of which 7 were waited for; matrix products, arithmetic and copies ran while one was open for 56% of the time, Pallas kernels for 0%

profile of v1, /device:TPU:0, one launch (start us, length us, event | category | flops | bytes accessed | tf_op | source)
XLA Modules:
  0.0 1893.9 jit_solution(16945096521603027842)
XLA Ops:
  13.8 7.5 all-to-all-start
  24.4 221.6 %all-gather = bf16[8,144,2]{1,2,0:T(2,128)(2,1)S(1)} all-gather(bf16[1,144,2]{1,2,0:T(2,128)(2,1)S(1)} %bitcast.234), channel_id=1, replica_groups=mesh['fsdp'=8,'seq'=4] {'fsdp'}, dimensions={0}, use_global_device_ids=true | all-gather | bytes 5184 | tf_op jit(solution)/shard_map/all_gather | solution.py:128
  247.1 164.3 %all-reduce.20 = (bf16[6912]{0:T(1024)(128)(2,1)S(1)}, bf16[1152]{0:T(1024)(128)(2,1)}, bf16[1152]{0:T(1024)(128)(2,1)}, bf16[4608]{0:T(1024)(128)(2,1)}) all-reduce(bf16[6912]{0:T(1024)(128)(2,1)S(1)} %dynamic-update-slice, bf16[1152]{0:T(1024)(128)(2,1)S(1)} %dynamic-update-slice.1, ...), channel_id=1, replica_groups=mesh['fsdp'=8,'seq'=4] {'fsdp'}, use_global_device_ids=true, to_apply=%add | all-reduce | flops 13824 | bytes 55296
  412.0 7.7 convolution_reduce_fusion
  420.5 6.0 fusion.74
  431.0 6.2 reduce.42
  443.9 6.2 reduce.43
  458.5 6.2 reduce.44
  473.0 6.4 all-to-all-done.3
  482.7 8.2 multiply_reduce_fusion
  490.9 8.5 exponential_reduce_fusion
  499.5 9.5 convolution_convert_fusion.4
  513.2 6.6 reduce.45
  528.6 8.3 all-to-all-done.4
  550.6 46.7 %all-gather.17.cloned.1.call-done = bf16[1152,4608]{1,0:T(8,128)(2,1)} async-done(((bf16[144,4608]{1,0:T(8,128)(2,1)}), bf16[1152,4608]{1,0:T(8,128)(2,1)}) %all-gather.17.cloned.1.call-update) | async-done | bytes 10616848 | tf_op jit(solution)/shard_map/all_gather | solution.py:131
  597.3 6.2 convolution_add_fusion
  605.9 9.3 fusion.52
  616.5 133.2 %all-gather.19.cloned.1.call-done = bf16[4608,1152]{1,0:T(8,128)(2,1)} async-done(((bf16[576,1152]{1,0:T(8,128)(2,1)}), bf16[4608,1152]{1,0:T(8,128)(2,1)}) %all-gather.19.cloned.1.call-update) | async-done | bytes 10616848 | tf_op jit(solution)/shard_map/all_gather | solution.py:133
  749.7 8.9 fusion.85
  758.6 8.9 fusion.34
  768.3 9.8 fusion.18
  784.6 8.1 reduce.46
  794.8 13.9 all_to_all.134
  817.3 9.6 convolution_convert_fusion.1
  831.4 7.4 reduce.47
  848.3 11.1 multiply_convert_fusion.1
  867.4 7.4 reduce.48
  882.6 5.7 convolution_convert_fusion.3
  891.2 6.7 reduce.49
  931.9 4.7 copy.141
  939.3 7.1 fusion.29
  952.8 6.6 multiply_convert_fusion
  964.3 9.2 fusion.39
  973.5 8.2 fusion.43
  981.7 639.3 %fusion.80 = (f32[48,3456]{1,0:T(8,128)S(1)}, f32[48,1152]{1,0:T(8,128)S(1)}, f32[40,4608]{1,0:T(8,128)S(1)}) fusion(f32[1152,3456]{1,0:T(8,128)} %fusion.43, f32[1152,1152]{1,0:T(8,128)} %fusion.57, f32[1152,4608]{1,0:T(8,128)} %fusion.39), kind=kCustom, calls=%all-reduce-scatter.3 | all-reduce-scatter fusion | flops 12976130 | bytes 44089344
  1632.5 16.8 concatenate.12
  1655.2 12.8 collective-permute-start.14
  1668.0 10.9 collective-permute-start.13
  1678.9 5.0 collective-permute-start.12
  1695.6 9.8 fusion.11
  1705.4 39.0 %all-reduce.19 = (bf16[6912]{0:T(1024)(128)(2,1)S(1)}, bf16[2,1152]{1,0:T(2,128)(2,1)S(1)}, bf16[1152]{0:T(1024)(128)(2,1)S(1)}, bf16[4608]{0:T(1024)(128)(2,1)S(1)}, bf16[1152]{0:T(1024)(128)(2,1)S(1)}) all-reduce(bf16[6912]{0:T(1024)(128)(2,1)S(1)} %copy-done.22, ...), channel_id=3, replica_groups=mesh['fsdp'=8,'seq'=4] {'fsdp','seq'}, use_global_device_ids=true, to_apply=%region_20.21.clone | all-reduce | flops 16128 | bytes 82944
  1748.8 4.9 collective-permute-start.11
  1759.1 5.0 all-gather.2
  1770.0 7.6 all-reduce.21
  1786.7 5.3 concatenate.11
  1801.4 28.3 %all-gather.3 = bf16[4,36,1152]{2,1,0:T(8,128)(2,1)S(1)} all-gather(bf16[1,36,1152]{2,1,0:T(8,128)(2,1)S(1)} %fusion.60), channel_id=1, replica_groups=mesh['fsdp'=8,'seq'=4] {'seq'}, dimensions={0}, use_global_device_ids=true | all-gather | bytes 414720 | tf_op jit(solution)/shard_map/all_gather | solution.py:262
  1830.6 33.7 %concatenate.10 = bf16[420,3456]{1,0:T(8,128)(2,1)} concatenate(bf16[36,3456]{1,0:T(8,128)(2,1)} %collective-permute-done.7, bf16[48,3456]{1,0:T(8,128)(2,1)S(1)} %collective-permute-done.6, bf16[48,3456]{1,0:T(8,128)(2,1)} %copy-done.18, bf16[48,3456]{1,0:T(8,128)(2,1)} %collective-permute-done.4, bf16[48,3456]{1,0:T(8,128)(2,1)} %collective-permute-done.3, ...), dimensions={0} | concatenate | bytes 6137856
  1865.4 10.3 all-gather.1
  (342 shorter events, 243.5 us)
Async XLA Ops:
  7.2 404.8 %all-gather.13.cloned.1.call-start = ((), (), s32[]{:S(2)}) async-start(), calls=%async_computation.11 | async-start | bytes 17915904 | tf_op jit(solution)/shard_map/all_gather | solution.py:140
  7.9 537.4 %all-gather.15.cloned.1.call-start = ((), (), s32[]{:S(2)}) async-start(), calls=%async_computation.12 | async-start | bytes 2985984 | tf_op jit(solution)/shard_map/all_gather | solution.py:129
  8.7 588.6 %all-gather.17.cloned.1.call-start = ((), (), s32[]{:S(2)}) async-start(), calls=%async_computation.13 | async-start | bytes 11943936 | tf_op jit(solution)/shard_map/all_gather | solution.py:131
  9.4 740.2 %all-gather.19.cloned.1.call-start = ((), (), s32[]{:S(2)}) async-start(), calls=%async_computation.14 | async-start | bytes 11943936 | tf_op jit(solution)/shard_map/all_gather | solution.py:133
  13.7 232.4 %copy-start.57 = (bf16[144]{0:T(256)(128)(2,1)S(1)}, bf16[144]{0:T(256)(128)(2,1)}, u32[]{:S(2)}) copy-start(bf16[144]{0:T(256)(128)(2,1)} %param.20) | copy-start | bytes 868
  13.7 232.7 %copy-start.58 = (bf16[144]{0:T(256)(128)(2,1)S(1)}, bf16[144]{0:T(256)(128)(2,1)}, u32[]{:S(2)}) copy-start(bf16[144]{0:T(256)(128)(2,1)} %param.24) | copy-start | bytes 868
  13.7 232.9 %copy-start.54 = (bf16[864]{0:T(1024)(128)(2,1)S(1)}, bf16[864]{0:T(1024)(128)(2,1)}, u32[]{:S(2)}) copy-start(bf16[864]{0:T(1024)(128)(2,1)} %param.16) | copy-start | bytes 5188
  13.7 233.1 %copy-start.55 = (bf16[576]{0:T(1024)(128)(2,1)S(1)}, bf16[576]{0:T(1024)(128)(2,1)}, u32[]{:S(2)}) copy-start(bf16[576]{0:T(1024)(128)(2,1)} %param.22) | copy-start | bytes 3460
  13.7 397.7 %copy-start.1 = (bf16[1,256,1152]{2,1,0:T(8,128)(2,1)S(1)}, bf16[1,256,1152]{2,1,0:T(8,128)(2,1)}, u32[]{:S(2)}) copy-start(bf16[1,256,1152]{2,1,0:T(8,128)(2,1)} %param.13) | copy-start | bytes 1769476
  13.8 398.3 %copy-start.28 = (f32[1,1152]{1,0:T(1,128)S(1)}, f32[1,1152]{1,0:T(1,128)}, u32[]{:S(2)}) copy-start(f32[1,1152]{1,0:T(1,128)} %param.14) | copy-start | bytes 13828
  13.8 406.7 %all-to-all-start = ((bf16[8,144,3456]{2,1,0:T(8,128)(2,1)}), bf16[8,144,3456]{2,1,0:T(8,128)(2,1)}, u32[]{:S(2)}, u32[]{:S(2)}) async-start(bf16[8,144,3456]{2,1,0:T(8,128)(2,1)} %stack.41), calls=%async_computation | async-start | bytes 15925248 | tf_op jit(solution)/shard_map/all_to_all | solution.py:126
  21.2 918.0 %all-gather.21.cloned.1.call-start = ((), (), s32[]{:S(2)}) async-start(), calls=%async_computation.15 | async-start | bytes 8957952 | tf_op jit(solution)/shard_map/all_gather | solution.py:185
  438.1 13.1 all-to-all-start.1
  451.3 14.4 all-to-all-start.2
  465.7 13.7 all-to-all-start.3
  523.2 13.7 all-to-all-start.4
  527.4 1163.3 %reduce-scatter.12.cloned.1.call-start = ((), (), s32[]{:S(2)}) async-start(), calls=%async_computation.18 | async-start | bytes 21897216 | tf_op jit(solution)/shard_map/reduce_scatter | solution.py:255
  842.2 36.0 %all-to-all-start.8 = ((bf16[4,2,36864]{2,1,0:T(2,128)(2,1)}), bf16[4,2,36864]{2,1,0:T(2,128)(2,1)}, u32[]{:S(2)}, u32[]{:S(2)}) async-start(bf16[4,2,36864]{2,1,0:T(2,128)(2,1)} %reshape.489), calls=%async_computation.8 | async-start | bytes 1179648 | tf_op jit(solution)/shard_map/all_to_all | solution.py:213
  878.2 21.7 %all-to-all-start.7 = ((bf16[4,2,36864]{2,1,0:T(2,128)(2,1)}), bf16[4,2,36864]{2,1,0:T(2,128)(2,1)}, u32[]{:S(2)}, u32[]{:S(2)}) async-start(bf16[4,2,36864]{2,1,0:T(2,128)(2,1)} %reshape.491), calls=%async_computation.7 | async-start | bytes 1179648 | tf_op jit(solution)/shard_map/all_to_all | solution.py:212
  899.9 28.0 %all-to-all-start.6 = ((bf16[4,2,36864]{2,1,0:T(2,128)(2,1)}), bf16[4,2,36864]{2,1,0:T(2,128)(2,1)}, u32[]{:S(2)}, u32[]{:S(2)}) async-start(bf16[4,2,36864]{2,1,0:T(2,128)(2,1)} %reshape.493), calls=%async_computation.6 | async-start | bytes 1179648 | tf_op jit(solution)/shard_map/all_to_all | solution.py:211
  904.1 887.9 %reduce-scatter.10.cloned.1.call-start = ((), (), s32[]{:S(2)}) async-start(), calls=%async_computation.16 | async-start | bytes 17915904 | tf_op jit(solution)/shard_map/reduce_scatter | solution.py:240
  959.4 917.6 %all-gather.25.cloned.1.call-start = ((), (), s32[]{:S(2)}) async-start(), calls=%async_computation.20 | async-start | bytes 1843200 | tf_op jit(solution)/shard_map/all_gather | solution.py:264
  1621.8 29.4 %copy-start.59 = (u32[32]{0:T(128)S(1)}, u32[32]{0:T(128)}, u32[]{:S(2)}) copy-start(u32[32]{0:T(128)} %constant.92) | copy-start | bytes 388
  1621.8 9.2 collective-permute-start.18
  1623.9 8.5 collective-permute-start.17
  1626.0 6.5 collective-permute-start.16
  1628.0 2.9 collective-permute-start.19
  1649.3 34.6 %copy-start.19 = (bf16[1,6,1152]{2,1,0:T(8,128)(2,1)S(1)}, bf16[1,6,1152]{2,1,0:T(8,128)(2,1)}, u32[]{:S(2)}) copy-start(bf16[1,6,1152]{2,1,0:T(8,128)(2,1)} %stack.48) | copy-start | bytes 41476
  1651.1 228.7 %all-gather.23.cloned.1.call-start = ((), (), s32[]{:S(2)}) async-start(), calls=%async_computation.19 | async-start | bytes 1658880 | tf_op jit(solution)/shard_map/all_gather | solution.py:266
  1654.5 38.1 %copy-start.38 = (f32[256]{0:T(256)S(1)}, f32[256]{0:T(256)}, u32[]{:S(2)}) copy-start(f32[256]{0:T(256)} %copy-done.36) | copy-start | bytes 3076
  1654.5 38.2 %copy-start.45 = (f32[256]{0:T(256)S(1)}, f32[256]{0:T(256)}, u32[]{:S(2)}) copy-start(f32[256]{0:T(256)} %copy-done.43) | copy-start | bytes 3076
  1655.2 93.6 %collective-permute-start.14 = (bf16[48,1152]{1,0:T(8,128)(2,1)S(1)}, bf16[48,1152]{1,0:T(8,128)(2,1)S(1)}, u32[]{:S(2)}, u32[]{:S(2)}) collective-permute-start(bf16[48,1152]{1,0:T(8,128)(2,1)S(1)} %convert.56), channel_id=1, source_target_pairs={{0,7},{1,8},{2,9},{3,10},{4,11},{5,12},{6,13},{7,14},{8,15},{9,16}... | collective-permute-start | bytes 331784
  1668.0 85.8 %collective-permute-start.13 = (bf16[48,1152]{1,0:T(8,128)(2,1)S(1)}, bf16[48,1152]{1,0:T(8,128)(2,1)}, u32[]{:S(2)}, u32[]{:S(2)}) collective-permute-start(bf16[48,1152]{1,0:T(8,128)(2,1)S(1)} %convert.56), channel_id=1, source_target_pairs={{0,6},{1,7},{2,8},{3,9},{4,10},{5,11},{6,12},{7,13},{8,14},{9,15},... | collective-permute-start | bytes 331784
  1678.9 76.2 %collective-permute-start.12 = (bf16[48,1152]{1,0:T(8,128)(2,1)S(1)}, bf16[48,1152]{1,0:T(8,128)(2,1)}, u32[]{:S(2)}, u32[]{:S(2)}) collective-permute-start(bf16[48,1152]{1,0:T(8,128)(2,1)S(1)} %convert.56), channel_id=1, source_target_pairs={{0,5},{1,6},{2,7},{3,8},{4,9},{5,10},{6,11},{7,12},{8,13},{9,14},{... | collective-permute-start | bytes 331784
  1685.1 110.5 %collective-permute-start.6 = (bf16[48,3456]{1,0:T(8,128)(2,1)S(1)}, bf16[48,3456]{1,0:T(8,128)(2,1)S(1)}, u32[]{:S(2)}, u32[]{:S(2)}) collective-permute-start(bf16[48,3456]{1,0:T(8,128)(2,1)S(1)} %convert.55), channel_id=1, source_target_pairs={{0,7},{1,8},{2,9},{3,10},{4,11},{5,12},{6,13},{7,14},{8,15},{9,16}... | collective-permute-start | bytes 995336
  1688.0 56.4 %collective-permute-start.15 = (bf16[36,1152]{1,0:T(8,128)(2,1)}, bf16[36,1152]{1,0:T(8,128)(2,1)S(1)}, u32[]{:S(2)}, u32[]{:S(2)}) collective-permute-start(bf16[36,1152]{1,0:T(8,128)(2,1)} %slice.57), channel_id=1, source_target_pairs={{0,8},{1,9},{2,10},{3,11},{4,12},{5,13},{6,14},{7,15},{8,16},{9,17... | collective-permute-start | bytes 248840
  1692.6 190.2 %all-reduce.25.cloned.1.call-start = ((), (), s32[]{:S(2)}) async-start(), calls=%async_computation.17 | async-start | bytes 3981312 | tf_op jit(solution)/shard_map/psum | solution.py:275
  1744.5 54.9 %collective-permute-start.5 = (bf16[48,3456]{1,0:T(8,128)(2,1)S(1)}, bf16[48,3456]{1,0:T(8,128)(2,1)S(1)}, u32[]{:S(2)}, u32[]{:S(2)}) collective-permute-start(bf16[48,3456]{1,0:T(8,128)(2,1)S(1)} %convert.55), channel_id=1, source_target_pairs={{0,6},{1,7},{2,8},{3,9},{4,10},{5,11},{6,12},{7,13},{8,14},{9,15},... | collective-permute-start | bytes 995336
  1748.8 15.3 collective-permute-start.11
  1753.8 12.8 collective-permute-start.10
  1755.1 36.9 %collective-permute-start.7 = (bf16[36,3456]{1,0:T(8,128)(2,1)}, bf16[36,3456]{1,0:T(8,128)(2,1)}, u32[]{:S(2)}, u32[]{:S(2)}) collective-permute-start(bf16[36,3456]{1,0:T(8,128)(2,1)} %slice.56), channel_id=1, source_target_pairs={{0,8},{1,9},{2,10},{3,11},{4,12},{5,13},{6,14},{7,15},{8,16},{9,17... | collective-permute-start | bytes 746504
  1764.1 17.1 collective-permute-start.9
  1766.6 16.6 collective-permute-start.8
  1781.2 49.4 %collective-permute-start.4 = (bf16[48,3456]{1,0:T(8,128)(2,1)S(1)}, bf16[48,3456]{1,0:T(8,128)(2,1)}, u32[]{:S(2)}, u32[]{:S(2)}) collective-permute-start(bf16[48,3456]{1,0:T(8,128)(2,1)S(1)} %convert.55), channel_id=1, source_target_pairs={{0,5},{1,6},{2,7},{3,8},{4,9},{5,10},{6,11},{7,12},{8,13},{9,14},{... | collective-permute-start | bytes 995336
  1783.9 46.7 %collective-permute-start.3 = (bf16[48,3456]{1,0:T(8,128)(2,1)S(1)}, bf16[48,3456]{1,0:T(8,128)(2,1)}, u32[]{:S(2)}, u32[]{:S(2)}) collective-permute-start(bf16[48,3456]{1,0:T(8,128)(2,1)S(1)} %convert.55), channel_id=1, source_target_pairs={{0,4},{1,5},{2,6},{3,7},{4,8},{5,9},{6,10},{7,11},{8,12},{9,13},{1... | collective-permute-start | bytes 995336
  1792.0 38.6 %collective-permute-start.2 = (bf16[48,3456]{1,0:T(8,128)(2,1)S(1)}, bf16[48,3456]{1,0:T(8,128)(2,1)S(1)}, u32[]{:S(2)}, u32[]{:S(2)}) collective-permute-start(bf16[48,3456]{1,0:T(8,128)(2,1)S(1)} %convert.55), channel_id=1, source_target_pairs={{0,3},{1,4},{2,5},{3,6},{4,7},{5,8},{6,9},{7,10},{8,11},{9,12},{10... | collective-permute-start | bytes 995336
  1795.6 35.1 %collective-permute-start.1 = (bf16[48,3456]{1,0:T(8,128)(2,1)S(1)}, bf16[48,3456]{1,0:T(8,128)(2,1)}, u32[]{:S(2)}, u32[]{:S(2)}) collective-permute-start(bf16[48,3456]{1,0:T(8,128)(2,1)S(1)} %convert.55), channel_id=1, source_target_pairs={{0,2},{1,3},{2,4},{3,5},{4,6},{5,7},{6,8},{7,9},{8,10},{9,11},{10,... | collective-permute-start | bytes 995336
  1799.3 31.3 %collective-permute-start = (bf16[48,3456]{1,0:T(8,128)(2,1)S(1)}, bf16[48,3456]{1,0:T(8,128)(2,1)}, u32[]{:S(2)}, u32[]{:S(2)}) collective-permute-start(bf16[48,3456]{1,0:T(8,128)(2,1)S(1)} %convert.55), channel_id=1, source_target_pairs={{0,1},{1,2},{2,3},{3,4},{4,5},{5,6},{6,7},{7,8},{8,9},{9,10},{10,1... | collective-permute-start | bytes 995336
  (51 other events, 430.9 us)
Sparse Core Ops, SparseCore 0:
  10.2 378.0 all-gather.12
  390.4 53.8 all-gather.14
  446.5 150.7 all-gather.16
  599.3 150.2 all-gather.18
  751.7 117.2 all-gather.20
  875.3 299.9 reduce-scatter.11
  1179.2 422.8 reduce-scatter.9
  1651.3 36.3 all-gather.24
  1692.7 22.5 all-gather.22
  1792.1 62.4 all-reduce.24
